TPU v7x, 32 devices: a whole 2x2x4 slice. The times are simulated.
32 devices in a mesh: wide: 8 (over y, x, core), narrow: 4 (over z).
Axes of the slice: x: 2, y: 2, z: 4, core: 2. Of those that a mesh axis runs over, the one named last changes fastest.
Arguments:
- tokens: bfloat16 [8192, 2048], P(('wide', 'narrow')), may hold values from -6 to 6
- out_grad: bfloat16 [8192, 2048], P(('wide', 'narrow')), may hold values from -6 to 6
- captions: bfloat16 [4096, 4096], P(('wide', 'narrow')), may hold values from -6 to 6
- image_blocks: int32 [32, 256], P('wide'), may hold values from 0 to 3, never falling along the last dimension, each value on 1 to 128 neighbouring positions
- caption_owner: int32 [8, 512], P('wide'), may hold values from 0 to 3, never falling along the last dimension, each value on 1 to 256 neighbouring positions
- norm_gains: float32 [3, 2048], replicated, may hold values from 0.25 to 1.75
- norm_shifts: float32 [3, 2048], replicated, may hold values from -3 to 3
- w_query: float32 [2048, 2048], P('wide', 'narrow'), may hold values from -0.125 to 0.125
- w_key: float32 [2048, 2048], P('wide', 'narrow'), may hold values from -0.125 to 0.125
- w_value: float32 [2048, 2048], P('wide', 'narrow'), may hold values from -0.125 to 0.125
- w_out: float32 [2048, 2048], P('narrow', 'wide'), may hold values from -0.375 to 0.375
- w_cross_query: float32 [2048, 2048], P('wide', 'narrow'), may hold values from -0.125 to 0.125
- w_cross_key: float32 [4096, 2048], P('wide', 'narrow'), may hold values from -0.09375 to 0.09375
- w_cross_value: float32 [4096, 2048], P('wide', 'narrow'), may hold values from -0.09375 to 0.09375
- w_cross_out: float32 [2048, 2048], P('narrow', 'wide'), may hold values from -0.375 to 0.375
- w_up: float32 [2048, 8192], P('wide', 'narrow'), may hold values from -0.125 to 0.125
- w_down: float32 [8192, 2048], P('narrow', 'wide'), may hold values from -0.0625 to 0.0625
Outputs:
- block_out: bfloat16 [8192, 2048], P(('wide', 'narrow'))
- grad_tokens: bfloat16 [8192, 2048], P(('wide', 'narrow'))
- grad_captions: bfloat16 [4096, 4096], P(('wide', 'narrow'))
- grad_norm_gains: float32 [3, 2048], replicated
- grad_norm_shifts: float32 [3, 2048], replicated
- grad_w_query: float32 [2048, 2048], P('wide', 'narrow')
- grad_w_key: float32 [2048, 2048], P('wide', 'narrow')
- grad_w_value: float32 [2048, 2048], P('wide', 'narrow')
- grad_w_out: float32 [2048, 2048], P('narrow', 'wide')
- grad_w_cross_query: float32 [2048, 2048], P('wide', 'narrow')
- grad_w_cross_key: float32 [4096, 2048], P('wide', 'narrow')
- grad_w_cross_value: float32 [4096, 2048], P('wide', 'narrow')
- grad_w_cross_out: float32 [2048, 2048], P('narrow', 'wide')
- grad_w_up: float32 [2048, 8192], P('wide', 'narrow')
- grad_w_down: float32 [8192, 2048], P('narrow', 'wide')
Inputs may be any that keep to these rules, and one draw needn't show every extreme that they name: `image_blocks`: within an image the block numbers never fall; each of the 4 blocks has 1 to 128 tokens, and one block of every image has exactly that many. `caption_owner`: within a group the owners never fall; every image of the group has 1 to 256 caption tokens, and one image of every group has exactly 256.
All inputs are finite; a program needn't handle non-finite values.
Results may differ from a plain program's by a relative error of at most 0.024.
Values may be sent and summed in bfloat16 or wider, within the bound.
A program may use at most 320 MiB of HBM per device.

v0:
```python
import jax
import jax.numpy as jnp
from jax import lax
from jax.sharding import PartitionSpec as P

HEAD_DIM = 128
PIX = 256
CHUNKS = 2
EPSILON = 1e-06
MASKED = -1000000000.0
BF = jnp.bfloat16
F32 = jnp.float32


def product(left_side, right_side):
    return lax.dot_general(
        left_side, right_side, (((left_side.ndim - 1,), (0,)), ((), ())), preferred_element_type=F32
    )


def right_inner(left_side, right_side):
    return lax.dot_general(
        left_side, right_side, (((left_side.ndim - 1,), (1,)), ((), ())), preferred_element_type=F32
    )


def left_inner(left_side, right_side):
    rows = tuple(range(left_side.ndim - 1))
    return lax.dot_general(
        left_side, right_side, ((rows, rows), ((), ())), preferred_element_type=F32
    )


def spread(rows):
    n = lax.axis_size("narrow")
    here = lax.axis_index("narrow")
    up, down = ([rows], [rows])
    for step in range(1, n):
        up.append(lax.ppermute(up[-1], "narrow", [(k, k + 1) for k in range(step - 1, n - 1)]))
        down.append(lax.ppermute(down[-1], "narrow", [(k, k - 1) for k in range(1, n - step + 1)]))
    parts = [rows] + [jnp.where(here >= s, up[s], down[n - s]) for s in range(1, n)]
    return jnp.stack(parts)


def sink(parts):
    n = lax.axis_size("narrow")
    up = down = None
    for step in range(1, n):
        one, other = (parts[step], parts[n - step])
        if up is not None:
            one = up.astype(F32) + one.astype(F32)
            other = down.astype(F32) + other.astype(F32)
        up = lax.ppermute(one.astype(BF), "narrow", [(k, k + 1) for k in range(step)])
        down = lax.ppermute(other.astype(BF), "narrow", [(k, k - 1) for k in range(n - step, n)])
    return up.astype(F32) + down.astype(F32) + parts[0].astype(F32)


def norm_stats(features):
    center = features - jnp.mean(features, axis=-1, keepdims=True)
    rstd = lax.rsqrt(jnp.mean(center * center, axis=-1, keepdims=True) + EPSILON)
    return (center * rstd, rstd)


def norm_back(grad, xhat, rstd, gain):
    scaled = grad * gain
    return rstd * (
        scaled
        - jnp.mean(scaled, axis=-1, keepdims=True)
        - xhat * jnp.mean(scaled * xhat, axis=-1, keepdims=True)
    )


def norm_sums(grad, xhat):
    return jnp.stack([jnp.sum(grad * xhat, axis=0), jnp.sum(grad, axis=0)])


def score_block(queries, keys_in, allowed, score_scale):
    raw = jnp.einsum("iphe,iqhe->ihpq", queries, keys_in, preferred_element_type=F32)
    return jnp.where(allowed[:, None], raw * score_scale, MASKED)


def attend(queries, keys_in, values_in, allowed, score_scale):
    scores = score_block(queries, keys_in, allowed, score_scale)
    log_total = jax.nn.logsumexp(scores, axis=-1, keepdims=True)
    soft = jnp.exp(scores - log_total).astype(BF)
    mixture = jnp.einsum("ihpq,iqhe->iphe", soft, values_in, preferred_element_type=F32)
    return (mixture.astype(BF), log_total)


def attend_back(queries, keys_in, values_in, allowed, log_total, grad_mix, score_scale):
    soft = jnp.exp(score_block(queries, keys_in, allowed, score_scale) - log_total)
    grad_soft = jnp.einsum("iphe,iqhe->ihpq", grad_mix, values_in, preferred_element_type=F32)
    grad_values = jnp.einsum(
        "ihpq,iphe->iqhe", soft.astype(BF), grad_mix, preferred_element_type=F32
    )
    row_dot = jnp.sum(soft * grad_soft, axis=-1, keepdims=True)
    grad_scores = (soft * (grad_soft - row_dot) * score_scale).astype(BF)
    grad_queries = jnp.einsum("ihpq,iqhe->iphe", grad_scores, keys_in, preferred_element_type=F32)
    grad_keys = jnp.einsum("ihpq,iphe->iqhe", grad_scores, queries, preferred_element_type=F32)
    return (grad_queries.astype(BF), grad_keys, grad_values)


def after(value, *others):
    return lax.optimization_barrier((value, *others))[0]


def follow(value, other):
    return value + (other[(0,) * other.ndim].astype(F32) * 0.0).astype(value.dtype)


def exchange_sum(value):
    for axis in ("wide", "narrow"):
        size = lax.axis_size(axis)
        step = 1
        while step < size:
            value = value + lax.ppermute(value, axis, [(k, k ^ step) for k in range(size)])
            step *= 2
    return value


def body(
    tokens,
    out_grad,
    captions,
    image_blocks,
    caption_owner,
    norm_gains,
    norm_shifts,
    w_query,
    w_key,
    w_value,
    w_out,
    w_cross_query,
    w_cross_key,
    w_cross_value,
    w_cross_out,
    w_up,
    w_down,
):
    scale = HEAD_DIM ** (-0.5)
    n = lax.axis_size("narrow")
    here = lax.axis_index("narrow")
    width = w_query.shape[1]
    heads = width // HEAD_DIM
    part = PIX // CHUNKS
    chunks = [slice(c * part, (c + 1) * part) for c in range(CHUNKS)]
    image_of = (here - jnp.arange(n)) % n

    def relative(blocks):
        return jnp.stack(
            [lax.dynamic_index_in_dim(blocks, image_of[s], 0, False) for s in range(n)]
        )

    def rows_of(*pieces):
        return lax.all_gather(
            jnp.concatenate([p.astype(BF) for p in pieces], axis=1), "wide", axis=0, tiled=True
        )

    def columns_of(piece):
        return lax.all_gather(piece.astype(BF), "wide", axis=1, tiled=True)

    def to_rows(g):
        return lax.psum_scatter(g.astype(BF), "wide", scatter_dimension=0, tiled=True).astype(F32)

    def to_columns(g):
        return lax.psum_scatter(g.astype(BF), "wide", scatter_dimension=1, tiled=True).astype(F32)

    full_qkv = rows_of(w_query, w_key, w_value)
    full_out = columns_of(w_out)
    full_ckv = rows_of(w_cross_key, w_cross_value)
    full_cq = rows_of(w_cross_query)
    full_cout = columns_of(w_cross_out)
    full_up = rows_of(w_up)
    full_down = columns_of(w_down)
    residual0 = tokens.astype(F32)
    xhat1, rstd1 = norm_stats(residual0)
    own1 = (xhat1 * norm_gains[0] + norm_shifts[0]).astype(BF)
    normed1 = spread(own1)
    qkv = product(normed1, full_qkv).astype(BF)
    heads_of = lambda x: x.reshape(x.shape[:-1] + (x.shape[-1] // HEAD_DIM, HEAD_DIM))
    self_q, self_k, self_v = [heads_of(qkv[..., k * width : (k + 1) * width]) for k in range(3)]
    blocks = image_blocks[image_of]
    self_allowed = blocks[:, :, None] == blocks[:, None, :]
    self_mix, self_total = attend(self_q, self_k, self_v, self_allowed, scale)
    self_mix = self_mix.reshape(n, PIX, width)
    text_rows = lax.all_gather(captions, "narrow", axis=0, tiled=True)
    text_count, text_width = text_rows.shape
    ckv = product(text_rows, full_ckv).astype(BF)
    cross_k = heads_of(ckv[None, :, :width])
    cross_v = heads_of(ckv[None, :, width:])
    owner = caption_owner[0]
    part_image = jnp.repeat(image_of, part)
    cross_allowed = (part_image[:, None] == owner[None, :])[None]
    state = []
    for rows in chunks:
        residual1 = residual0[rows] + sink(product(self_mix[:, rows], full_out).astype(BF))
        xhat2, rstd2 = norm_stats(residual1)
        state.append((residual1, xhat2, rstd2))
    normed2 = [spread((s[1] * norm_gains[1] + norm_shifts[1]).astype(BF)) for s in state]
    grad_all = relative(lax.all_gather(out_grad, "narrow", axis=0))
    cross_q, cross_mix, cross_total, state3 = ([], [], [], [])
    for c in range(CHUNKS):
        q = heads_of(product(normed2[c], full_cq).astype(BF).reshape(1, n * part, width))
        mix, total = attend(q, cross_k, cross_v, cross_allowed, scale)
        mix = mix.reshape(n, part, width)
        residual2 = state[c][0] + sink(product(mix, full_cout).astype(BF))
        xhat3, rstd3 = norm_stats(residual2)
        cross_q.append(q)
        cross_mix.append(mix)
        cross_total.append(total)
        state3.append((residual2, xhat3, rstd3))
    normed3 = [spread((s[1] * norm_gains[2] + norm_shifts[2]).astype(BF)) for s in state3]
    out_parts, acts, grad_hiddens, grad2, sums3 = ([], [], [], [], [])
    for c, rows in enumerate(chunks):
        if c > 0:
            normed3[c] = follow(normed3[c], sent)
        hidden = product(normed3[c], full_up)
        grad_rows = grad_all[:, rows]
        acted, gelu_back = jax.vjp(jax.nn.gelu, hidden)
        acted = acted.astype(BF)
        grad_hidden = gelu_back(right_inner(grad_rows, full_down))[0].astype(BF)
        acts.append(acted)
        grad_hiddens.append(grad_hidden)
        sent = lax.optimization_barrier(right_inner(grad_hidden, full_up).astype(BF))
        grad_n3 = sink(sent)
        residual2, xhat3, rstd3 = state3[c]
        sums3.append(norm_sums(grad_n3, xhat3))
        grad2.append(out_grad[rows].astype(F32) + norm_back(grad_n3, xhat3, rstd3, norm_gains[2]))
        out_parts.append(product(acted, full_down).astype(BF))
    cat = lambda xs: jnp.concatenate(xs, axis=1)
    acted, grad_hidden, n3 = (cat(acts), cat(grad_hiddens), cat(normed3))
    grad_down = left_inner(acted, cat([grad_all[:, rows] for rows in chunks]))
    grad_up = left_inner(n3, grad_hidden)
    out_sum = lax.psum_scatter(relative(cat(out_parts)), "narrow", scatter_dimension=0)
    block_out = (jnp.concatenate([s[0] for s in state3]) + out_sum.astype(F32)).astype(BF)
    e2 = [spread(g.astype(BF)) for g in grad2]
    own_down = to_columns(grad_down)
    own_up = to_rows(grad_up)
    e2[-1] = after(e2[-1], grad_down, grad_up)
    grad1, sums2, grad_cqs, grad_ck, grad_cv = ([], [], [], 0.0, 0.0)
    for c in range(CHUNKS):
        grad_mix = heads_of(right_inner(e2[c], full_cout).astype(BF).reshape(1, n * part, width))
        gq, gk, gv = attend_back(
            cross_q[c], cross_k, cross_v, cross_allowed, cross_total[c], grad_mix, scale
        )
        gq = gq.reshape(n, part, width)
        grad_cqs.append(gq)
        grad_ck = grad_ck + gk
        grad_cv = grad_cv + gv
        grad_n2 = sink(right_inner(gq, full_cq).astype(BF))
        _, xhat2, rstd2 = state[c]
        sums2.append(norm_sums(grad_n2, xhat2))
        grad1.append(grad2[c] + norm_back(grad_n2, xhat2, rstd2, norm_gains[1]))
    grad_cout = left_inner(cat(cross_mix), cat(e2))
    grad_cq = left_inner(cat(normed2), cat(grad_cqs))
    grad_ckv = jnp.concatenate(
        [grad_ck.reshape(text_count, width), grad_cv.reshape(text_count, width)], axis=1
    ).astype(BF)
    grad_text_part = right_inner(grad_ckv, full_ckv).astype(BF).reshape(n, -1, text_width)
    grad_wckv = left_inner(text_rows, grad_ckv)
    e1 = [spread(g.astype(BF)) for g in grad1]
    own_cout = to_columns(grad_cout)
    own_cq = to_rows(grad_cq)
    own_ckv = to_rows(grad_wckv)
    e1[-1] = after(e1[-1], grad_cout, grad_cq, grad_wckv, grad_text_part)
    grad_mix = heads_of(cat([right_inner(e, full_out).astype(BF) for e in e1]))
    grad_mix = after(grad_mix, own_down, own_up)
    gq, gk, gv = attend_back(self_q, self_k, self_v, self_allowed, self_total, grad_mix, scale)
    grad_qkv = jnp.concatenate([g.astype(BF).reshape(n, PIX, width) for g in (gq, gk, gv)], axis=-1)
    grad_out = left_inner(self_mix, cat(e1))
    grad_wqkv = left_inner(normed1, grad_qkv)
    grad_n1 = sink(right_inner(after(grad_qkv, grad_wqkv), full_qkv).astype(BF))
    grad_text = sink(relative(after(grad_text_part, grad_mix))).astype(BF)
    grad1 = jnp.concatenate(grad1)
    grad_n1 = after(grad_n1, own_cout, own_cq, own_ckv)
    grad_tokens = (grad1 + norm_back(grad_n1, xhat1, rstd1, norm_gains[0])).astype(BF)
    sums = exchange_sum(jnp.stack([norm_sums(grad_n1, xhat1), sum(sums2), sum(sums3)]))
    own_out = to_columns(grad_out)
    own_qkv = to_rows(grad_wqkv)
    return (
        block_out,
        grad_tokens,
        grad_text,
        sums[:, 0],
        sums[:, 1],
        own_qkv[:, :width],
        own_qkv[:, width : 2 * width],
        own_qkv[:, 2 * width :],
        own_out,
        own_cq,
        own_ckv[:, :width],
        own_ckv[:, width:],
        own_cout,
        own_up,
        own_down,
    )


def solution(mesh):
    in_specs = (
        P(("wide", "narrow"), None),
        P(("wide", "narrow"), None),
        P(("wide", "narrow"), None),
        P("wide", None),
        P("wide", None),
        P(),
        P(),
        P("wide", "narrow"),
        P("wide", "narrow"),
        P("wide", "narrow"),
        P("narrow", "wide"),
        P("wide", "narrow"),
        P("wide", "narrow"),
        P("wide", "narrow"),
        P("narrow", "wide"),
        P("wide", "narrow"),
        P("narrow", "wide"),
    )
    out_specs = (
        P(("wide", "narrow"), None),
        P(("wide", "narrow"), None),
        P(("wide", "narrow"), None),
        P(),
        P(),
        P("wide", "narrow"),
        P("wide", "narrow"),
        P("wide", "narrow"),
        P("narrow", "wide"),
        P("wide", "narrow"),
        P("wide", "narrow"),
        P("wide", "narrow"),
        P("narrow", "wide"),
        P("wide", "narrow"),
        P("narrow", "wide"),
    )
    return jax.shard_map(body, mesh=mesh, in_specs=in_specs, out_specs=out_specs, check_vma=False)
```

profile of v0, /device:TPU:0, one launch (start us, length us, event | category | flops | bytes accessed | tf_op | source)
XLA Modules:
  0.0 1377.7 jit_solution(2369147938922174307)
XLA Ops:
  28.0 21.0 %collective-permute-done = bf16[256,2048]{1,0:T(8,128)(2,1)S(1)} collective-permute-done((bf16[256,2048]{1,0:T(8,128)(2,1)S(1)}, bf16[256,2048]{1,0:T(8,128)(2,1)S(1)}, u32[]{:S(2)}, u32[]{:S(2)}) %collective-permute-start) | collective-permute-done | bytes 1048608 | tf_op jit(solution)/shard_map/ppermute | solution.py:39
  57.5 22.6 %collective-permute-done.2 = bf16[256,2048]{1,0:T(8,128)(2,1)} collective-permute-done((bf16[256,2048]{1,0:T(8,128)(2,1)S(1)}, bf16[256,2048]{1,0:T(8,128)(2,1)}, u32[]{:S(2)}, u32[]{:S(2)}) %collective-permute-start.2) | collective-permute-done | bytes 1048608 | tf_op jit(solution)/shard_map/ppermute | solution.py:40
  85.7 19.9 %collective-permute-done.3 = bf16[256,2048]{1,0:T(8,128)(2,1)S(1)} collective-permute-done((bf16[256,2048]{1,0:T(8,128)(2,1)}, bf16[256,2048]{1,0:T(8,128)(2,1)S(1)}, u32[]{:S(2)}, u32[]{:S(2)}) %collective-permute-start.3) | collective-permute-done | bytes 1048608 | tf_op jit(solution)/shard_map/ppermute | solution.py:40
  106.6 9.4 fusion.91
  133.5 18.8 %collective-permute-done.6 = bf16[128,2048]{1,0:T(8,128)(2,1)S(1)} collective-permute-done((bf16[128,2048]{1,0:T(8,128)(2,1)S(1)}, bf16[128,2048]{1,0:T(8,128)(2,1)S(1)}, u32[]{:S(2)}, u32[]{:S(2)}) %collective-permute-start.6) | collective-permute-done | bytes 524320 | tf_op jit(solution)/shard_map/ppermute | solution.py:53
  157.7 17.1 %collective-permute-done.24 = bf16[128,2048]{1,0:T(8,128)(2,1)S(1)} collective-permute-done((bf16[128,2048]{1,0:T(8,128)(2,1)S(1)}, bf16[128,2048]{1,0:T(8,128)(2,1)S(1)}, u32[]{:S(2)}, u32[]{:S(2)}) %collective-permute-start.24) | collective-permute-done | bytes 524320 | tf_op jit(solution)/shard_map/ppermute | solution.py:53
  180.2 17.0 %collective-permute-done.7 = bf16[128,2048]{1,0:T(8,128)(2,1)S(1)} collective-permute-done((bf16[128,2048]{1,0:T(8,128)(2,1)S(1)}, bf16[128,2048]{1,0:T(8,128)(2,1)S(1)}, u32[]{:S(2)}, u32[]{:S(2)}) %collective-permute-start.7) | collective-permute-done | bytes 524320 | tf_op jit(solution)/shard_map/ppermute | solution.py:53
  203.4 16.4 %collective-permute-done.25 = bf16[128,2048]{1,0:T(8,128)(2,1)S(1)} collective-permute-done((bf16[128,2048]{1,0:T(8,128)(2,1)S(1)}, bf16[128,2048]{1,0:T(8,128)(2,1)S(1)}, u32[]{:S(2)}, u32[]{:S(2)}) %collective-permute-start.25) | collective-permute-done | bytes 524320 | tf_op jit(solution)/shard_map/ppermute | solution.py:53
  226.3 15.9 %collective-permute-done.8 = bf16[128,2048]{1,0:T(8,128)(2,1)S(1)} collective-permute-done((bf16[128,2048]{1,0:T(8,128)(2,1)S(1)}, bf16[128,2048]{1,0:T(8,128)(2,1)S(1)}, u32[]{:S(2)}, u32[]{:S(2)}) %collective-permute-start.8) | collective-permute-done | bytes 524320 | tf_op jit(solution)/shard_map/ppermute | solution.py:53
  242.2 19.3 %collective-permute-done.26 = bf16[128,2048]{1,0:T(8,128)(2,1)S(1)} collective-permute-done((bf16[128,2048]{1,0:T(8,128)(2,1)S(1)}, bf16[128,2048]{1,0:T(8,128)(2,1)S(1)}, u32[]{:S(2)}, u32[]{:S(2)}) %collective-permute-start.26) | collective-permute-done | bytes 524320 | tf_op jit(solution)/shard_map/ppermute | solution.py:53
  282.2 9.1 collective-permute-done.31
  338.4 9.5 fusion.222
  373.6 19.3 %collective-permute-done.18 = bf16[128,2048]{1,0:T(8,128)(2,1)S(1)} collective-permute-done((bf16[128,2048]{1,0:T(8,128)(2,1)S(1)}, bf16[128,2048]{1,0:T(8,128)(2,1)S(1)}, u32[]{:S(2)}, u32[]{:S(2)}) %collective-permute-start.18) | collective-permute-done | bytes 524320 | tf_op jit(solution)/shard_map/ppermute | solution.py:53
  398.4 17.0 %collective-permute-done.36 = bf16[128,2048]{1,0:T(8,128)(2,1)S(1)} collective-permute-done((bf16[128,2048]{1,0:T(8,128)(2,1)S(1)}, bf16[128,2048]{1,0:T(8,128)(2,1)S(1)}, u32[]{:S(2)}, u32[]{:S(2)}) %collective-permute-start.36) | collective-permute-done | bytes 524320 | tf_op jit(solution)/shard_map/ppermute | solution.py:53
  420.8 17.0 %collective-permute-done.19 = bf16[128,2048]{1,0:T(8,128)(2,1)S(1)} collective-permute-done((bf16[128,2048]{1,0:T(8,128)(2,1)S(1)}, bf16[128,2048]{1,0:T(8,128)(2,1)S(1)}, u32[]{:S(2)}, u32[]{:S(2)}) %collective-permute-start.19) | collective-permute-done | bytes 524320 | tf_op jit(solution)/shard_map/ppermute | solution.py:53
  444.0 16.4 %collective-permute-done.37 = bf16[128,2048]{1,0:T(8,128)(2,1)S(1)} collective-permute-done((bf16[128,2048]{1,0:T(8,128)(2,1)S(1)}, bf16[128,2048]{1,0:T(8,128)(2,1)S(1)}, u32[]{:S(2)}, u32[]{:S(2)}) %collective-permute-start.37) | collective-permute-done | bytes 524320 | tf_op jit(solution)/shard_map/ppermute | solution.py:53
  466.4 15.7 %collective-permute-done.20 = bf16[128,2048]{1,0:T(8,128)(2,1)S(1)} collective-permute-done((bf16[128,2048]{1,0:T(8,128)(2,1)S(1)}, bf16[128,2048]{1,0:T(8,128)(2,1)S(1)}, u32[]{:S(2)}, u32[]{:S(2)}) %collective-permute-start.20) | collective-permute-done | bytes 524320 | tf_op jit(solution)/shard_map/ppermute | solution.py:53
  482.8 14.0 %collective-permute-done.38 = bf16[128,2048]{1,0:T(8,128)(2,1)S(1)} collective-permute-done((bf16[128,2048]{1,0:T(8,128)(2,1)S(1)}, bf16[128,2048]{1,0:T(8,128)(2,1)S(1)}, u32[]{:S(2)}, u32[]{:S(2)}) %collective-permute-start.38) | collective-permute-done | bytes 524320 | tf_op jit(solution)/shard_map/ppermute | solution.py:53
  540.2 9.5 collective-permute-done.44
  563.9 11.9 multiply_convert_fusion.4
  575.8 32.7 %all-gather.25.cloned.1.call-done = bf16[2048,2048]{1,0:T(8,128)(2,1)} async-done(((bf16[2048,256]{1,0:T(8,128)(2,1)}), bf16[2048,2048]{1,0:T(8,128)(2,1)}) %all-gather.25.cloned.1.call-update) | async-done | bytes 8388624 | tf_op jit(solution)/shard_map/all_gather | solution.py:160
  608.5 10.5 fusion.29
  627.7 10.1 multiply_convert_fusion.3
  646.2 13.5 convolution_bitcast_fusion.2
  659.7 14.4 %convolution_bitcast_fusion.3 = bf16[2048,2048]{1,0:T(8,128)(2,1)} fusion(bf16[4,128,2048]{2,1,0:T(8,128)(2,1)} %get-tuple-element.189, bf16[4,128,2048]{2,1,0:T(8,128)(2,1)} %get-tuple-element.187, bf16[1,256,2048]{2,1,0:T(8,128)(2,1)} %copy-done.45, bf16[1,256,2048]{2,1,0:T(8,128)(2,1)} %copy-done.46, bf16[1,256,2048]{2,1,0:T(8,128)(2,1)} %copy-done.47, ...), kind=kOutput, calls=%fused_computation.7 | convolution fusion | flops 8604614656 | bytes 16777216 | tf_op jit(solution)/shard_map/dot_general | solution.py:29
  736.0 10.8 collective-permute-done.74
  769.6 9.9 collective-permute-done.79
  792.1 9.9 collective-permute-done.80
  804.9 18.6 %collective-permute-done.81 = bf16[128,2048]{1,0:T(8,128)(2,1)S(1)} collective-permute-done((bf16[128,2048]{1,0:T(8,128)(2,1)S(1)}, bf16[128,2048]{1,0:T(8,128)(2,1)S(1)}, u32[]{:S(2)}, u32[]{:S(2)}) %collective-permute-start.81) | collective-permute-done | bytes 524320 | tf_op jit(solution)/shard_map/ppermute | solution.py:40
  842.5 9.4 fusion.265
  856.0 9.7 fusion.262
  932.9 10.6 collective-permute-start.85
  947.9 20.0 %collective-permute-start.68 = (bf16[128,2048]{1,0:T(8,128)(2,1)}, bf16[128,2048]{1,0:T(8,128)(2,1)}, u32[]{:S(2)}, u32[]{:S(2)}) collective-permute-start(bf16[128,2048]{1,0:T(8,128)(2,1)} %get-tuple-element.99), channel_id=1, source_target_pairs={{0,1},{1,2},{2,3},{4,5},{5,6},{6,7},{8,9},{9,10},{10,11},{12,13},{... | collective-permute-start | bytes 1572872 | tf_op jit(solution)/shard_map/ppermute | solution.py:53
  969.3 10.3 fusion.226
  981.3 11.5 collective-permute-start.86
  996.2 16.9 %collective-permute-done.86 = bf16[128,2048]{1,0:T(8,128)(2,1)S(1)} collective-permute-done((bf16[128,2048]{1,0:T(8,128)(2,1)S(1)}, bf16[128,2048]{1,0:T(8,128)(2,1)S(1)}, u32[]{:S(2)}, u32[]{:S(2)}) %collective-permute-start.86) | collective-permute-done | bytes 524320 | tf_op jit(solution)/shard_map/ppermute | solution.py:53
  1019.9 25.2 %collective-permute-start.96 = (bf16[128,2048]{1,0:T(8,128)(2,1)S(1)}, bf16[128,2048]{1,0:T(8,128)(2,1)S(1)}, u32[]{:S(2)}, u32[]{:S(2)}) collective-permute-start(bf16[128,2048]{1,0:T(8,128)(2,1)S(1)} %get-tuple-element.68), channel_id=1, source_target_pairs={{0,1},{1,2},{2,3},{4,5},{5,6},{6,7},{8,9},{9,10},{10,11},{12,13},{... | collective-permute-start | bytes 1572872 | tf_op jit(solution)/shard_map/ppermute | solution.py:39
  1069.4 10.2 convolution_convert_fusion
  1088.5 11.1 collective-permute-done.99
  1135.6 9.9 fusion.219
  1147.0 9.9 fusion.216
  1170.6 10.6 fusion.94
  1189.1 17.9 %collective-permute-done.102 = bf16[256,2048]{1,0:T(8,128)(2,1)S(1)} collective-permute-done((bf16[256,2048]{1,0:T(8,128)(2,1)S(1)}, bf16[256,2048]{1,0:T(8,128)(2,1)S(1)}, u32[]{:S(2)}, u32[]{:S(2)}) %collective-permute-start.102) | collective-permute-done | bytes 1048608 | tf_op jit(solution)/shard_map/ppermute | solution.py:53
  1219.3 10.2 collective-permute-done.108
  1237.7 14.3 %collective-permute-done.103 = bf16[256,2048]{1,0:T(8,128)(2,1)} collective-permute-done((bf16[256,2048]{1,0:T(8,128)(2,1)}, bf16[256,2048]{1,0:T(8,128)(2,1)}, u32[]{:S(2)}, u32[]{:S(2)}) %collective-permute-start.103) | collective-permute-done | bytes 1048608 | tf_op jit(solution)/shard_map/ppermute | solution.py:53
  1284.8 12.2 collective-permute-done.104
  1321.9 19.2 %collective-permute-start.118 = (f32[3,2,2048]{2,0,1:T(4,128)S(1)}, f32[3,2,2048]{2,0,1:T(4,128)S(1)}, u32[]{:S(2)}, u32[]{:S(2)}) collective-permute-start(f32[3,2,2048]{2,0,1:T(4,128)S(1)} %add.569), channel_id=1, source_target_pairs={{0,2},{1,3},{2,0},{3,1},{4,6},{5,7},{6,4},{7,5},{8,10},{9,11},{10,... | collective-permute-start | bytes 147464 | tf_op jit(solution)/shard_map/ppermute | solution.py:116
  1344.0 20.7 %collective-permute-done.118 = f32[3,2,2048]{2,0,1:T(4,128)S(1)} collective-permute-done((f32[3,2,2048]{2,0,1:T(4,128)S(1)}, f32[3,2,2048]{2,0,1:T(4,128)S(1)}, u32[]{:S(2)}, u32[]{:S(2)}) %collective-permute-start.118) | collective-permute-done | bytes 49184 | tf_op jit(solution)/shard_map/ppermute | solution.py:116
  (758 shorter events, 644.8 us)
Async XLA Ops:
  7.2 99.4 %all-gather.11.cloned.1.call-start = ((), (), s32[]{:S(2)}) async-start(), calls=%async_computation.8 | async-start | bytes 7077888 | tf_op jit(solution)/shard_map/all_gather | solution.py:155
  11.6 112.8 %all-gather.13.cloned.1.call-start = ((), (), s32[]{:S(2)}) async-start(), calls=%async_computation.9 | async-start | bytes 2359296 | tf_op jit(solution)/shard_map/all_gather | solution.py:160
  12.4 310.2 %all-gather.19.cloned.1.call-start = ((), (), s32[]{:S(2)}) async-start(), calls=%async_computation.12 | async-start | bytes 2359296 | tf_op jit(solution)/shard_map/all_gather | solution.py:155
  13.2 325.2 %all-gather.17.cloned.1.call-start = ((), (), s32[]{:S(2)}) async-start(), calls=%async_computation.11 | async-start | bytes 5242880 | tf_op jit(solution)/shard_map/all_gather | solution.py:186
  13.8 324.6 %all-gather.15.cloned.1.call-start = ((), (), s32[]{:S(2)}) async-start(), calls=%async_computation.10 | async-start | bytes 9437184 | tf_op jit(solution)/shard_map/all_gather | solution.py:155
  16.5 346.2 %all-gather.21.cloned.1.call-start = ((), (), s32[]{:S(2)}) async-start(), calls=%async_computation.13 | async-start | bytes 2359296 | tf_op jit(solution)/shard_map/all_gather | solution.py:160
  18.4 507.8 %all-gather.27.cloned.1.call-start = ((), (), s32[]{:S(2)}) async-start(), calls=%async_computation.24 | async-start | bytes 5242880 | tf_op jit(solution)/shard_map/all_gather | solution.py:200
  19.2 544.7 %all-gather.23.cloned.1.call-start = ((), (), s32[]{:S(2)}) async-start(), calls=%async_computation.14 | async-start | bytes 9437184 | tf_op jit(solution)/shard_map/all_gather | solution.py:155
  20.4 588.1 %all-gather.25.cloned.1.call-start = ((), (), s32[]{:S(2)}) async-start(), calls=%async_computation.15 | async-start | bytes 9437184 | tf_op jit(solution)/shard_map/all_gather | solution.py:160
  131.5 43.3 %collective-permute-start.24 = (bf16[128,2048]{1,0:T(8,128)(2,1)S(1)}, bf16[128,2048]{1,0:T(8,128)(2,1)S(1)}, u32[]{:S(2)}, u32[]{:S(2)}) collective-permute-start(bf16[128,2048]{1,0:T(8,128)(2,1)S(1)} %get-tuple-element.147), channel_id=1, source_target_pairs={{0,1},{4,5},{8,9},{12,13},{16,17},{20,21},{24,25},{28,29}} | collective-permute-start | bytes 1572872 | tf_op jit(solution)/shard_map/ppermute | solution.py:53
  132.8 42.0 %collective-permute-start.27 = (bf16[128,2048]{1,0:T(8,128)(2,1)S(1)}, bf16[128,2048]{1,0:T(8,128)(2,1)S(1)}, u32[]{:S(2)}, u32[]{:S(2)}) collective-permute-start(bf16[128,2048]{1,0:T(8,128)(2,1)S(1)} %get-tuple-element.148), channel_id=1, source_target_pairs={{3,2},{7,6},{11,10},{15,14},{19,18},{23,22},{27,26},{31,30}} | collective-permute-start | bytes 1572872 | tf_op jit(solution)/shard_map/ppermute | solution.py:54
  152.6 44.7 %collective-permute-start.7 = (bf16[128,2048]{1,0:T(8,128)(2,1)S(1)}, bf16[128,2048]{1,0:T(8,128)(2,1)S(1)}, u32[]{:S(2)}, u32[]{:S(2)}) collective-permute-start(bf16[128,2048]{1,0:T(8,128)(2,1)S(1)} %get-tuple-element.139), channel_id=1, source_target_pairs={{0,1},{1,2},{4,5},{5,6},{8,9},{9,10},{12,13},{13,14},{16,17},{17,1... | collective-permute-start | bytes 1572872 | tf_op jit(solution)/shard_map/ppermute | solution.py:53
  157.0 40.2 %collective-permute-start.10 = (bf16[128,2048]{1,0:T(8,128)(2,1)S(1)}, bf16[128,2048]{1,0:T(8,128)(2,1)S(1)}, u32[]{:S(2)}, u32[]{:S(2)}) collective-permute-start(bf16[128,2048]{1,0:T(8,128)(2,1)S(1)} %get-tuple-element.140), channel_id=1, source_target_pairs={{2,1},{3,2},{6,5},{7,6},{10,9},{11,10},{14,13},{15,14},{18,17},{19... | collective-permute-start | bytes 1572872 | tf_op jit(solution)/shard_map/ppermute | solution.py:54
  175.1 44.6 %collective-permute-start.25 = (bf16[128,2048]{1,0:T(8,128)(2,1)S(1)}, bf16[128,2048]{1,0:T(8,128)(2,1)S(1)}, u32[]{:S(2)}, u32[]{:S(2)}) collective-permute-start(bf16[128,2048]{1,0:T(8,128)(2,1)S(1)} %get-tuple-element.145), channel_id=1, source_target_pairs={{0,1},{1,2},{4,5},{5,6},{8,9},{9,10},{12,13},{13,14},{16,17},{17,1... | collective-permute-start | bytes 1572872 | tf_op jit(solution)/shard_map/ppermute | solution.py:53
  179.5 40.2 %collective-permute-start.28 = (bf16[128,2048]{1,0:T(8,128)(2,1)S(1)}, bf16[128,2048]{1,0:T(8,128)(2,1)S(1)}, u32[]{:S(2)}, u32[]{:S(2)}) collective-permute-start(bf16[128,2048]{1,0:T(8,128)(2,1)S(1)} %get-tuple-element.146), channel_id=1, source_target_pairs={{2,1},{3,2},{6,5},{7,6},{10,9},{11,10},{14,13},{15,14},{18,17},{19... | collective-permute-start | bytes 1572872 | tf_op jit(solution)/shard_map/ppermute | solution.py:54
  197.7 44.5 %collective-permute-start.8 = (bf16[128,2048]{1,0:T(8,128)(2,1)S(1)}, bf16[128,2048]{1,0:T(8,128)(2,1)S(1)}, u32[]{:S(2)}, u32[]{:S(2)}) collective-permute-start(bf16[128,2048]{1,0:T(8,128)(2,1)S(1)} %get-tuple-element.137), channel_id=1, source_target_pairs={{0,1},{1,2},{2,3},{4,5},{5,6},{6,7},{8,9},{9,10},{10,11},{12,13},{... | collective-permute-start | bytes 1572872 | tf_op jit(solution)/shard_map/ppermute | solution.py:53
  202.1 40.1 %collective-permute-start.11 = (bf16[128,2048]{1,0:T(8,128)(2,1)S(1)}, bf16[128,2048]{1,0:T(8,128)(2,1)S(1)}, u32[]{:S(2)}, u32[]{:S(2)}) collective-permute-start(bf16[128,2048]{1,0:T(8,128)(2,1)S(1)} %get-tuple-element.138), channel_id=1, source_target_pairs={{1,0},{2,1},{3,2},{5,4},{6,5},{7,6},{9,8},{10,9},{11,10},{13,12},{... | collective-permute-start | bytes 1572872 | tf_op jit(solution)/shard_map/ppermute | solution.py:54
  220.1 41.4 %collective-permute-start.26 = (bf16[128,2048]{1,0:T(8,128)(2,1)S(1)}, bf16[128,2048]{1,0:T(8,128)(2,1)S(1)}, u32[]{:S(2)}, u32[]{:S(2)}) collective-permute-start(bf16[128,2048]{1,0:T(8,128)(2,1)S(1)} %get-tuple-element.143), channel_id=1, source_target_pairs={{0,1},{1,2},{2,3},{4,5},{5,6},{6,7},{8,9},{9,10},{10,11},{12,13},{... | collective-permute-start | bytes 1572872 | tf_op jit(solution)/shard_map/ppermute | solution.py:53
  279.0 839.9 %reduce-scatter.13.cloned.1.call-start = ((), (), s32[]{:S(2)}) async-start(), calls=%async_computation.18 | async-start | bytes 9437184 | tf_op jit(solution)/shard_map/reduce_scatter | solution.py:163
  371.6 43.8 %collective-permute-start.36 = (bf16[128,2048]{1,0:T(8,128)(2,1)S(1)}, bf16[128,2048]{1,0:T(8,128)(2,1)S(1)}, u32[]{:S(2)}, u32[]{:S(2)}) collective-permute-start(bf16[128,2048]{1,0:T(8,128)(2,1)S(1)} %get-tuple-element.133), channel_id=1, source_target_pairs={{0,1},{4,5},{8,9},{12,13},{16,17},{20,21},{24,25},{28,29}} | collective-permute-start | bytes 1572872 | tf_op jit(solution)/shard_map/ppermute | solution.py:53
  372.9 42.5 %collective-permute-start.39 = (bf16[128,2048]{1,0:T(8,128)(2,1)S(1)}, bf16[128,2048]{1,0:T(8,128)(2,1)S(1)}, u32[]{:S(2)}, u32[]{:S(2)}) collective-permute-start(bf16[128,2048]{1,0:T(8,128)(2,1)S(1)} %get-tuple-element.134), channel_id=1, source_target_pairs={{3,2},{7,6},{11,10},{15,14},{19,18},{23,22},{27,26},{31,30}} | collective-permute-start | bytes 1572872 | tf_op jit(solution)/shard_map/ppermute | solution.py:54
  393.2 44.6 %collective-permute-start.19 = (bf16[128,2048]{1,0:T(8,128)(2,1)S(1)}, bf16[128,2048]{1,0:T(8,128)(2,1)S(1)}, u32[]{:S(2)}, u32[]{:S(2)}) collective-permute-start(bf16[128,2048]{1,0:T(8,128)(2,1)S(1)} %get-tuple-element.125), channel_id=1, source_target_pairs={{0,1},{1,2},{4,5},{5,6},{8,9},{9,10},{12,13},{13,14},{16,17},{17,1... | collective-permute-start | bytes 1572872 | tf_op jit(solution)/shard_map/ppermute | solution.py:53
  397.7 40.2 %collective-permute-start.22 = (bf16[128,2048]{1,0:T(8,128)(2,1)S(1)}, bf16[128,2048]{1,0:T(8,128)(2,1)S(1)}, u32[]{:S(2)}, u32[]{:S(2)}) collective-permute-start(bf16[128,2048]{1,0:T(8,128)(2,1)S(1)} %get-tuple-element.126), channel_id=1, source_target_pairs={{2,1},{3,2},{6,5},{7,6},{10,9},{11,10},{14,13},{15,14},{18,17},{19... | collective-permute-start | bytes 1572872 | tf_op jit(solution)/shard_map/ppermute | solution.py:54
  415.7 44.6 %collective-permute-start.37 = (bf16[128,2048]{1,0:T(8,128)(2,1)S(1)}, bf16[128,2048]{1,0:T(8,128)(2,1)S(1)}, u32[]{:S(2)}, u32[]{:S(2)}) collective-permute-start(bf16[128,2048]{1,0:T(8,128)(2,1)S(1)} %get-tuple-element.131), channel_id=1, source_target_pairs={{0,1},{1,2},{4,5},{5,6},{8,9},{9,10},{12,13},{13,14},{16,17},{17,1... | collective-permute-start | bytes 1572872 | tf_op jit(solution)/shard_map/ppermute | solution.py:53
  420.1 40.2 %collective-permute-start.40 = (bf16[128,2048]{1,0:T(8,128)(2,1)S(1)}, bf16[128,2048]{1,0:T(8,128)(2,1)S(1)}, u32[]{:S(2)}, u32[]{:S(2)}) collective-permute-start(bf16[128,2048]{1,0:T(8,128)(2,1)S(1)} %get-tuple-element.132), channel_id=1, source_target_pairs={{2,1},{3,2},{6,5},{7,6},{10,9},{11,10},{14,13},{15,14},{18,17},{19... | collective-permute-start | bytes 1572872 | tf_op jit(solution)/shard_map/ppermute | solution.py:54
  438.2 43.9 %collective-permute-start.20 = (bf16[128,2048]{1,0:T(8,128)(2,1)S(1)}, bf16[128,2048]{1,0:T(8,128)(2,1)S(1)}, u32[]{:S(2)}, u32[]{:S(2)}) collective-permute-start(bf16[128,2048]{1,0:T(8,128)(2,1)S(1)} %get-tuple-element.123), channel_id=1, source_target_pairs={{0,1},{1,2},{2,3},{4,5},{5,6},{6,7},{8,9},{9,10},{10,11},{12,13},{... | collective-permute-start | bytes 1572872 | tf_op jit(solution)/shard_map/ppermute | solution.py:53
  442.7 39.5 %collective-permute-start.23 = (bf16[128,2048]{1,0:T(8,128)(2,1)S(1)}, bf16[128,2048]{1,0:T(8,128)(2,1)S(1)}, u32[]{:S(2)}, u32[]{:S(2)}) collective-permute-start(bf16[128,2048]{1,0:T(8,128)(2,1)S(1)} %get-tuple-element.124), channel_id=1, source_target_pairs={{1,0},{2,1},{3,2},{5,4},{6,5},{7,6},{9,8},{10,9},{11,10},{13,12},{... | collective-permute-start | bytes 1572872 | tf_op jit(solution)/shard_map/ppermute | solution.py:54
  538.9 86.1 %collective-permute-start.51 = (bf16[128,2048]{1,0:T(8,128)(2,1)}, bf16[128,2048]{1,0:T(8,128)(2,1)}, u32[]{:S(2)}, u32[]{:S(2)}) collective-permute-start(bf16[128,2048]{1,0:T(8,128)(2,1)} %collective-permute-done.50), channel_id=1, source_target_pairs={{1,0},{5,4},{9,8},{13,12},{17,16},{21,20},{25,24},{29,28}} | collective-permute-start | bytes 1572872 | tf_op jit(solution)/shard_map/ppermute | solution.py:40
  552.9 73.3 %collective-permute-start.53 = (bf16[128,2048]{1,0:T(8,128)(2,1)}, bf16[128,2048]{1,0:T(8,128)(2,1)}, u32[]{:S(2)}, u32[]{:S(2)}) collective-permute-start(bf16[128,2048]{1,0:T(8,128)(2,1)} %collective-permute-done.52), channel_id=1, source_target_pairs={{2,3},{6,7},{10,11},{14,15},{18,19},{22,23},{26,27},{30,31}} | collective-permute-start | bytes 1572872 | tf_op jit(solution)/shard_map/ppermute | solution.py:39
  659.7 462.1 %reduce-scatter.11.cloned.1.call-start = ((), (), s32[]{:S(2)}) async-start(), calls=%async_computation.17 | async-start | bytes 9437184 | tf_op jit(solution)/shard_map/reduce_scatter | solution.py:166
  674.2 541.5 %reduce-scatter.15.cloned.1.call-start = ((), (), s32[]{:S(2)}) async-start(), calls=%async_computation.19 | async-start | bytes 2359296 | tf_op jit(solution)/shard_map/reduce_scatter | solution.py:166
  829.3 388.2 %reduce-scatter.17.cloned.1.call-start = ((), (), s32[]{:S(2)}) async-start(), calls=%async_computation.20 | async-start | bytes 2359296 | tf_op jit(solution)/shard_map/reduce_scatter | solution.py:163
  872.6 389.6 %reduce-scatter.9.cloned.1.call-start = ((), (), s32[]{:S(2)}) async-start(), calls=%async_computation.16 | async-start | bytes 5242880 | tf_op jit(solution)/shard_map/reduce_scatter | solution.py:234
  893.2 371.6 %reduce-scatter.23.cloned.1.call-start = ((), (), s32[]{:S(2)}) async-start(), calls=%async_computation.23 | async-start | bytes 2359296 | tf_op jit(solution)/shard_map/reduce_scatter | solution.py:166
  932.9 46.7 %collective-permute-start.85 = (bf16[128,2048]{1,0:T(8,128)(2,1)}, bf16[128,2048]{1,0:T(8,128)(2,1)}, u32[]{:S(2)}, u32[]{:S(2)}) collective-permute-start(bf16[128,2048]{1,0:T(8,128)(2,1)} %get-tuple-element.113), channel_id=1, source_target_pairs={{0,1},{1,2},{4,5},{5,6},{8,9},{9,10},{12,13},{13,14},{16,17},{17,1... | collective-permute-start | bytes 1572872 | tf_op jit(solution)/shard_map/ppermute | solution.py:53
  947.9 46.2 %collective-permute-start.68 = (bf16[128,2048]{1,0:T(8,128)(2,1)}, bf16[128,2048]{1,0:T(8,128)(2,1)}, u32[]{:S(2)}, u32[]{:S(2)}) collective-permute-start(bf16[128,2048]{1,0:T(8,128)(2,1)} %get-tuple-element.99), channel_id=1, source_target_pairs={{0,1},{1,2},{2,3},{4,5},{5,6},{6,7},{8,9},{9,10},{10,11},{12,13},{... | collective-permute-start | bytes 1572872 | tf_op jit(solution)/shard_map/ppermute | solution.py:53
  1018.5 39.3 %collective-permute-start.97 = (bf16[128,2048]{1,0:T(8,128)(2,1)S(1)}, bf16[128,2048]{1,0:T(8,128)(2,1)S(1)}, u32[]{:S(2)}, u32[]{:S(2)}) collective-permute-start(bf16[128,2048]{1,0:T(8,128)(2,1)S(1)} %get-tuple-element.68), channel_id=1, source_target_pairs={{1,0},{2,1},{3,2},{5,4},{6,5},{7,6},{9,8},{10,9},{11,10},{13,12},{... | collective-permute-start | bytes 1572872 | tf_op jit(solution)/shard_map/ppermute | solution.py:40
  1019.9 39.1 %collective-permute-start.96 = (bf16[128,2048]{1,0:T(8,128)(2,1)S(1)}, bf16[128,2048]{1,0:T(8,128)(2,1)S(1)}, u32[]{:S(2)}, u32[]{:S(2)}) collective-permute-start(bf16[128,2048]{1,0:T(8,128)(2,1)S(1)} %get-tuple-element.68), channel_id=1, source_target_pairs={{0,1},{1,2},{2,3},{4,5},{5,6},{6,7},{8,9},{9,10},{10,11},{12,13},{... | collective-permute-start | bytes 1572872 | tf_op jit(solution)/shard_map/ppermute | solution.py:39
  1111.2 189.2 %reduce-scatter.19.cloned.1.call-start = ((), (), s32[]{:S(2)}) async-start(), calls=%async_computation.21 | async-start | bytes 9437184 | tf_op jit(solution)/shard_map/reduce_scatter | solution.py:163
  1111.8 256.9 %reduce-scatter.21.cloned.1.call-start = ((), (), s32[]{:S(2)}) async-start(), calls=%async_computation.22 | async-start | bytes 7077888 | tf_op jit(solution)/shard_map/reduce_scatter | solution.py:163
  1186.6 43.0 %collective-permute-start.108 = (bf16[128,4096]{1,0:T(8,128)(2,1)}, bf16[128,4096]{1,0:T(8,128)(2,1)}, u32[]{:S(2)}, u32[]{:S(2)}) collective-permute-start(bf16[128,4096]{1,0:T(8,128)(2,1)} %dynamic-slice_bitcast_fusion.1), channel_id=1, source_target_pairs={{0,1},{4,5},{8,9},{12,13},{16,17},{20,21},{24,25},{28,29}} | collective-permute-start | bytes 3145736 | tf_op jit(solution)/shard_map/ppermute | solution.py:53
  1208.6 43.4 %collective-permute-start.103 = (bf16[256,2048]{1,0:T(8,128)(2,1)}, bf16[256,2048]{1,0:T(8,128)(2,1)}, u32[]{:S(2)}, u32[]{:S(2)}) collective-permute-start(bf16[256,2048]{1,0:T(8,128)(2,1)} %get-tuple-element.84), channel_id=1, source_target_pairs={{0,1},{1,2},{4,5},{5,6},{8,9},{9,10},{12,13},{13,14},{16,17},{17,1... | collective-permute-start | bytes 3145736 | tf_op jit(solution)/shard_map/ppermute | solution.py:53
  1214.0 38.1 %collective-permute-start.106 = (bf16[256,2048]{1,0:T(8,128)(2,1)S(1)}, bf16[256,2048]{1,0:T(8,128)(2,1)}, u32[]{:S(2)}, u32[]{:S(2)}) collective-permute-start(bf16[256,2048]{1,0:T(8,128)(2,1)S(1)} %get-tuple-element.85), channel_id=1, source_target_pairs={{2,1},{3,2},{6,5},{7,6},{10,9},{11,10},{14,13},{15,14},{18,17},{19... | collective-permute-start | bytes 3145736 | tf_op jit(solution)/shard_map/ppermute | solution.py:54
  1232.3 42.2 %collective-permute-start.109 = (bf16[128,4096]{1,0:T(8,128)(2,1)}, bf16[128,4096]{1,0:T(8,128)(2,1)}, u32[]{:S(2)}, u32[]{:S(2)}) collective-permute-start(bf16[128,4096]{1,0:T(8,128)(2,1)} %fusion.150), channel_id=1, source_target_pairs={{0,1},{1,2},{4,5},{5,6},{8,9},{9,10},{12,13},{13,14},{16,17},{17,1... | collective-permute-start | bytes 3145736 | tf_op jit(solution)/shard_map/ppermute | solution.py:53
  1256.5 40.5 %collective-permute-start.104 = (bf16[256,2048]{1,0:T(8,128)(2,1)}, bf16[256,2048]{1,0:T(8,128)(2,1)S(1)}, u32[]{:S(2)}, u32[]{:S(2)}) collective-permute-start(bf16[256,2048]{1,0:T(8,128)(2,1)} %get-tuple-element.82), channel_id=1, source_target_pairs={{0,1},{1,2},{2,3},{4,5},{5,6},{6,7},{8,9},{9,10},{10,11},{12,13},{... | collective-permute-start | bytes 3145736 | tf_op jit(solution)/shard_map/ppermute | solution.py:53
  1277.7 87.7 %collective-permute-start.110 = (bf16[128,4096]{1,0:T(8,128)(2,1)}, bf16[128,4096]{1,0:T(8,128)(2,1)}, u32[]{:S(2)}, u32[]{:S(2)}) collective-permute-start(bf16[128,4096]{1,0:T(8,128)(2,1)} %get-tuple-element.64), channel_id=1, source_target_pairs={{0,1},{1,2},{2,3},{4,5},{5,6},{6,7},{8,9},{9,10},{10,11},{12,13},{... | collective-permute-start | bytes 3145736 | tf_op jit(solution)/shard_map/ppermute | solution.py:53
  1318.8 46.6 %collective-permute-start.113 = (bf16[128,4096]{1,0:T(8,128)(2,1)}, bf16[128,4096]{1,0:T(8,128)(2,1)}, u32[]{:S(2)}, u32[]{:S(2)}) collective-permute-start(bf16[128,4096]{1,0:T(8,128)(2,1)} %add_convert_fusion), channel_id=1, source_target_pairs={{1,0},{2,1},{3,2},{5,4},{6,5},{7,6},{9,8},{10,9},{11,10},{13,12},{... | collective-permute-start | bytes 3145736 | tf_op jit(solution)/shard_map/ppermute | solution.py:54
  1321.9 42.8 %collective-permute-start.118 = (f32[3,2,2048]{2,0,1:T(4,128)S(1)}, f32[3,2,2048]{2,0,1:T(4,128)S(1)}, u32[]{:S(2)}, u32[]{:S(2)}) collective-permute-start(f32[3,2,2048]{2,0,1:T(4,128)S(1)} %add.569), channel_id=1, source_target_pairs={{0,2},{1,3},{2,0},{3,1},{4,6},{5,7},{6,4},{7,5},{8,10},{9,11},{10,... | collective-permute-start | bytes 147464 | tf_op jit(solution)/shard_map/ppermute | solution.py:116
  (228 other events, 5218.6 us)
Sparse Core Ops, SparseCore 0:
  11.7 48.1 all-gather.10
  62.3 28.0 all-gather.12
  92.9 27.7 all-gather.18
  122.2 140.3 all-gather.16
  264.8 56.8 all-gather.14
  323.5 28.0 all-gather.20
  353.2 138.1 all-gather.26
  493.9 56.2 all-gather.22
  552.6 55.8 all-gather.24
  659.8 71.4 reduce-scatter.12
  734.8 71.2 reduce-scatter.10
  829.4 46.3 reduce-scatter.14
  879.1 41.1 reduce-scatter.16
  922.4 120.6 reduce-scatter.8
  1111.3 42.6 reduce-scatter.22
  1157.3 71.3 reduce-scatter.18
  1231.9 61.7 reduce-scatter.20
where the time goes:
time: 1390 us; the launch traced here: 1380 us
  waiting for transfers between devices  580 us (42%)
  starting transfers between devices  322 us (23%)
  matrix products  290 us (21%)
  other arithmetic  112 us (8%)
  local copies, waits for them, and re-layouts  48 us (3%)
  between operations  25.5 us (2%)
    ppermute x30, waiting for transfers between devices, sink(): lax.ppermute(one.astype(BF), 'narrow', [(k, k + 1) for k in range(step)])  320 us
    ppermute x27, waiting for transfers between devices, spread(): lax.ppermute(down[-1], 'narrow', [(k, k - 1) for k in range(1, n - step +...  177 us
    ppermute x30, starting transfers between devices, sink(): lax.ppermute(one.astype(BF), 'narrow', [(k, k + 1) for k in range(step)])  142 us
    ppermute x27, starting transfers between devices, spread(): lax.ppermute(up[-1], 'narrow', [(k, k + 1) for k in range(step - 1, n - 1)])  86.5 us
    dot_general x12, matrix products, product(): lax.dot_general(left_side, right_side, (((left_side.ndim - 1,), (0,)), ((...  75.1 us
    dot_general x12, matrix products, right_inner(): lax.dot_general(left_side, right_side, (((left_side.ndim - 1,), (1,)), ((...  69.7 us
    dot_general x7, matrix products, left_inner(): lax.dot_general(left_side, right_side, ((rows, rows), ((), ())), preferre...  57.3 us
    ppermute x27, starting transfers between devices, spread(): lax.ppermute(down[-1], 'narrow', [(k, k - 1) for k in range(1, n - step +...  35.1 us
  transfers between devices with their start and end apart: 136, of which 51 were waited for; matrix products, arithmetic and copies ran while one was open for 29% of the time, Pallas kernels for 0%

commit v1 on v0

--- a/solution.py
+++ b/solution.py
@@ -10,6 +10,27 @@
 MASKED = -1000000000.0
 BF = jnp.bfloat16
 F32 = jnp.float32
+
+
+def ring_gather(shard, axis, dim):
+    peers, index, span = (lax.axis_size(axis), lax.axis_index(axis), shard.shape[dim])
+    right = [(i, (i + 1) % peers) for i in range(peers)]
+    left = [(i, (i - 1) % peers) for i in range(peers)]
+    out = jnp.zeros((*shard.shape[:dim], peers * span, *shard.shape[dim + 1 :]), shard.dtype)
+    out = lax.dynamic_update_slice_in_dim(out, shard, index * span, axis=dim)
+    from_left = from_right = shard
+    middle = peers // 2
+    for step in range(1, middle + 1):
+        from_left = lax.ppermute(from_left, axis, right)
+        out = lax.dynamic_update_slice_in_dim(
+            out, from_left, (index - step) % peers * span, axis=dim
+        )
+        if step < peers - middle:
+            from_right = lax.ppermute(from_right, axis, left)
+            out = lax.dynamic_update_slice_in_dim(
+                out, from_right, (index + step) % peers * span, axis=dim
+            )
+    return out
 
 
 def product(left_side, right_side):
@@ -157,7 +178,7 @@
         )
 
     def columns_of(piece):
-        return lax.all_gather(piece.astype(BF), "wide", axis=1, tiled=True)
+        return ring_gather(piece.astype(BF), "wide", 1)
 
     def to_rows(g):
         return lax.psum_scatter(g.astype(BF), "wide", scatter_dimension=0, tiled=True).astype(F32)

time: 1390 us -> 1410 us (1.014)
  waiting for transfers between devices: 580 us -> 535 us
  starting transfers between devices: 322 us -> 355 us
  local copies, waits for them, and re-layouts: 48 us -> 76.4 us
    ppermute x30, waiting for transfers between devices: 320 us -> 188 us  [sink(): lax.ppermute(one.astype(BF), 'narrow', [(k, k + 1) for k in range(step)])]
    ppermute x0 -> x21, waiting for transfers between devices: none -> 62.2 us  [the longest x9 43.9 us: ring_gather(): from_right = lax.ppermute(from_right, axis, left)]
    ppermute x27, waiting for transfers between devices: 177 us -> 233 us  [spread(): lax.ppermute(down[-1], 'narrow', [(k, k - 1) for k in range(1, n - step +...]
    all_gather x3 -> x0, waiting for transfers between devices: 32.8 us -> none  [columns_of(): return lax.all_gather(piece.astype(BF), 'wide', axis=1, tiled=True)]
    ppermute x0 -> x21, starting transfers between devices: none -> 25.9 us  [the longest x9 18.8 us: ring_gather(): from_right = lax.ppermute(from_right, axis, left)]
    dynamic_update_slice x0 -> x21, local copies, waits for them, and re-layouts: none -> 23.2 us  [the longest x12 13.1 us: ring_gather(): lax.dynamic_update_slice_in_dim(out, from_left, (index - step) % peers *...]
  transfers between devices with their start and end apart: 136 -> 154, of which waited for: 51 -> 59; matrix products, arithmetic and copies ran while one was open for 29% -> 31% of each run, Pallas kernels for 0% -> 0%
where the time goes in v1:
time: 1410 us; the launch traced here: 1400 us
  waiting for transfers between devices  535 us (38%)
  starting transfers between devices  355 us (25%)
  matrix products  285 us (20%)
  other arithmetic  120 us (9%)
  local copies, waits for them, and re-layouts  76.4 us (5%)
  between operations  26 us (2%)
    ppermute x27, waiting for transfers between devices, spread(): lax.ppermute(down[-1], 'narrow', [(k, k - 1) for k in range(1, n - step +...  233 us
    ppermute x30, waiting for transfers between devices, sink(): lax.ppermute(one.astype(BF), 'narrow', [(k, k + 1) for k in range(step)])  188 us
    ppermute x30, starting transfers between devices, sink(): lax.ppermute(one.astype(BF), 'narrow', [(k, k + 1) for k in range(step)])  146 us
    ppermute x27, starting transfers between devices, spread(): lax.ppermute(up[-1], 'narrow', [(k, k + 1) for k in range(step - 1, n - 1)])  89.4 us
    dot_general x12, matrix products, right_inner(): lax.dot_general(left_side, right_side, (((left_side.ndim - 1,), (1,)), ((...  70.2 us
    dot_general x12, matrix products, product(): lax.dot_general(left_side, right_side, (((left_side.ndim - 1,), (0,)), ((...  69.6 us
    dot_general x7, matrix products, left_inner(): lax.dot_general(left_side, right_side, ((rows, rows), ((), ())), preferre...  55.8 us
    ppermute x9, waiting for transfers between devices, ring_gather(): from_right = lax.ppermute(from_right, axis, left)  43.9 us
  transfers between devices with their start and end apart: 154, of which 59 were waited for; matrix products, arithmetic and copies ran while one was open for 31% of the time, Pallas kernels for 0%

profile of v1, /device:TPU:0, one launch (start us, length us, event | category | flops | bytes accessed | tf_op | source)
XLA Modules:
  0.0 1397.4 jit_solution(8932732362972261087)
XLA Ops:
  53.2 9.8 collective-permute-done.8
  87.4 19.5 %collective-permute-done.3 = bf16[256,2048]{1,0:T(8,128)(2,1)S(1)} collective-permute-done((bf16[256,2048]{1,0:T(8,128)(2,1)}, bf16[256,2048]{1,0:T(8,128)(2,1)S(1)}, u32[]{:S(2)}, u32[]{:S(2)}) %collective-permute-start.3) | collective-permute-done | bytes 1048608 | tf_op jit(solution)/shard_map/ppermute | solution.py:61
  108.0 10.9 fusion.91
  138.8 20.7 %collective-permute-done.13 = bf16[128,2048]{1,0:T(8,128)(2,1)S(1)} collective-permute-done((bf16[128,2048]{1,0:T(8,128)(2,1)S(1)}, bf16[128,2048]{1,0:T(8,128)(2,1)S(1)}, u32[]{:S(2)}, u32[]{:S(2)}) %collective-permute-start.13) | collective-permute-done | bytes 524320 | tf_op jit(solution)/shard_map/ppermute | solution.py:74
  167.6 14.4 %collective-permute-done.38 = bf16[128,2048]{1,0:T(8,128)(2,1)S(1)} collective-permute-done((bf16[128,2048]{1,0:T(8,128)(2,1)S(1)}, bf16[128,2048]{1,0:T(8,128)(2,1)S(1)}, u32[]{:S(2)}, u32[]{:S(2)}) %collective-permute-start.38) | collective-permute-done | bytes 524320 | tf_op jit(solution)/shard_map/ppermute | solution.py:74
  210.6 12.3 collective-permute-done.39
  252.4 38.2 %collective-permute-done.28 = bf16[512,256]{1,0:T(8,128)(2,1)S(1)} collective-permute-done((bf16[512,256]{1,0:T(8,128)(2,1)S(1)}, bf16[512,256]{1,0:T(8,128)(2,1)S(1)}, u32[]{:S(2)}, u32[]{:S(2)}) %collective-permute-start.28) | collective-permute-done | bytes 262176 | tf_op jit(solution)/shard_map/ppermute | solution.py:29
  325.1 22.0 %collective-permute-done.21 = bf16[128,2048]{1,0:T(8,128)(2,1)S(1)} collective-permute-done((bf16[128,2048]{1,0:T(8,128)(2,1)S(1)}, bf16[128,2048]{1,0:T(8,128)(2,1)S(1)}, u32[]{:S(2)}, u32[]{:S(2)}) %collective-permute-start.21) | collective-permute-done | bytes 524320 | tf_op jit(solution)/shard_map/ppermute | solution.py:61
  353.4 24.6 %collective-permute-done.46 = bf16[128,2048]{1,0:T(8,128)(2,1)S(1)} collective-permute-done((bf16[128,2048]{1,0:T(8,128)(2,1)S(1)}, bf16[128,2048]{1,0:T(8,128)(2,1)S(1)}, u32[]{:S(2)}, u32[]{:S(2)}) %collective-permute-start.46) | collective-permute-done | bytes 524320 | tf_op jit(solution)/shard_map/ppermute | solution.py:61
  380.1 38.9 %collective-permute-done.22 = bf16[128,2048]{1,0:T(8,128)(2,1)S(1)} collective-permute-done((bf16[128,2048]{1,0:T(8,128)(2,1)S(1)}, bf16[128,2048]{1,0:T(8,128)(2,1)S(1)}, u32[]{:S(2)}, u32[]{:S(2)}) %collective-permute-start.22) | collective-permute-done | bytes 524320 | tf_op jit(solution)/shard_map/ppermute | solution.py:61
  421.4 9.2 collective-permute-done.47
  443.4 9.2 fusion.222
  506.0 8.2 collective-permute-start.34
  585.2 9.9 collective-permute-done.58
  602.5 15.1 %collective-permute-done.59 = bf16[128,2048]{1,0:T(8,128)(2,1)S(1)} collective-permute-done((bf16[128,2048]{1,0:T(8,128)(2,1)}, bf16[128,2048]{1,0:T(8,128)(2,1)S(1)}, u32[]{:S(2)}, u32[]{:S(2)}) %collective-permute-start.59) | collective-permute-done | bytes 524320 | tf_op jit(solution)/shard_map/ppermute | solution.py:61
  620.5 10.8 multiply_convert_fusion.4
  631.2 9.2 fusion.29
  655.8 9.7 fusion.36
  666.9 12.2 convolution_bitcast_fusion.2
  679.1 14.3 %convolution_bitcast_fusion.3 = bf16[2048,2048]{1,0:T(8,128)(2,1)} fusion(bf16[4,128,2048]{2,1,0:T(8,128)(2,1)} %get-tuple-element.195, bf16[4,128,2048]{2,1,0:T(8,128)(2,1)} %get-tuple-element.193, bf16[1,256,2048]{2,1,0:T(8,128)(2,1)} %copy-done.45, bf16[1,256,2048]{2,1,0:T(8,128)(2,1)} %copy-done.46, bf16[1,256,2048]{2,1,0:T(8,128)(2,1)} %copy-done.47, ...), kind=kOutput, calls=%fused_computation.7 | convolution fusion | flops 8604614656 | bytes 16777216 | tf_op jit(solution)/shard_map/dot_general | solution.py:50
  698.0 9.3 fusion.117
  756.0 10.6 collective-permute-done.95
  789.5 9.9 collective-permute-done.100
  812.0 9.9 collective-permute-done.101
  824.8 18.9 %collective-permute-done.102 = bf16[128,2048]{1,0:T(8,128)(2,1)S(1)} collective-permute-done((bf16[128,2048]{1,0:T(8,128)(2,1)S(1)}, bf16[128,2048]{1,0:T(8,128)(2,1)S(1)}, u32[]{:S(2)}, u32[]{:S(2)}) %collective-permute-start.102) | collective-permute-done | bytes 524320 | tf_op jit(solution)/shard_map/ppermute | solution.py:61
  859.4 9.4 fusion.265
  872.8 10.0 fusion.262
  889.9 8.8 fusion.120
  898.7 8.2 fusion.123
  938.3 8.5 fusion.131
  949.2 12.8 collective-permute-start.106
  966.3 13.3 collective-permute-start.89
  981.1 10.4 fusion.226
  993.3 15.2 %collective-permute-start.107 = (bf16[128,2048]{1,0:T(8,128)(2,1)S(1)}, bf16[128,2048]{1,0:T(8,128)(2,1)S(1)}, u32[]{:S(2)}, u32[]{:S(2)}) collective-permute-start(bf16[128,2048]{1,0:T(8,128)(2,1)S(1)} %get-tuple-element.117), channel_id=1, source_target_pairs={{0,1},{1,2},{2,3},{4,5},{5,6},{6,7},{8,9},{9,10},{10,11},{12,13},{... | collective-permute-start | bytes 1572872 | tf_op jit(solution)/shard_map/ppermute | solution.py:74
  1011.9 16.2 %collective-permute-done.107 = bf16[128,2048]{1,0:T(8,128)(2,1)S(1)} collective-permute-done((bf16[128,2048]{1,0:T(8,128)(2,1)S(1)}, bf16[128,2048]{1,0:T(8,128)(2,1)S(1)}, u32[]{:S(2)}, u32[]{:S(2)}) %collective-permute-start.107) | collective-permute-done | bytes 524320 | tf_op jit(solution)/shard_map/ppermute | solution.py:74
  1034.8 30.0 %collective-permute-start.117 = (bf16[128,2048]{1,0:T(8,128)(2,1)S(1)}, bf16[128,2048]{1,0:T(8,128)(2,1)S(1)}, u32[]{:S(2)}, u32[]{:S(2)}) collective-permute-start(bf16[128,2048]{1,0:T(8,128)(2,1)S(1)} %get-tuple-element.68), channel_id=1, source_target_pairs={{0,1},{1,2},{2,3},{4,5},{5,6},{6,7},{8,9},{9,10},{10,11},{12,13},{... | collective-permute-start | bytes 1572872 | tf_op jit(solution)/shard_map/ppermute | solution.py:60
  1089.3 10.1 convolution_convert_fusion
  1111.4 9.1 collective-permute-done.120
  1155.3 9.8 fusion.219
  1166.5 9.7 fusion.216
  1181.1 8.9 convolution_bitcast_fusion
  1190.0 10.8 fusion.94
  1208.6 18.1 %collective-permute-done.123 = bf16[256,2048]{1,0:T(8,128)(2,1)S(1)} collective-permute-done((bf16[256,2048]{1,0:T(8,128)(2,1)S(1)}, bf16[256,2048]{1,0:T(8,128)(2,1)S(1)}, u32[]{:S(2)}, u32[]{:S(2)}) %collective-permute-start.123) | collective-permute-done | bytes 1048608 | tf_op jit(solution)/shard_map/ppermute | solution.py:74
  1239.1 10.1 collective-permute-done.129
  1257.4 14.3 %collective-permute-done.124 = bf16[256,2048]{1,0:T(8,128)(2,1)} collective-permute-done((bf16[256,2048]{1,0:T(8,128)(2,1)}, bf16[256,2048]{1,0:T(8,128)(2,1)}, u32[]{:S(2)}, u32[]{:S(2)}) %collective-permute-start.124) | collective-permute-done | bytes 1048608 | tf_op jit(solution)/shard_map/ppermute | solution.py:74
  1304.4 12.2 collective-permute-done.125
  1341.6 19.2 %collective-permute-start.139 = (f32[3,2,2048]{2,0,1:T(4,128)S(1)}, f32[3,2,2048]{2,0,1:T(4,128)S(1)}, u32[]{:S(2)}, u32[]{:S(2)}) collective-permute-start(f32[3,2,2048]{2,0,1:T(4,128)S(1)} %add.682), channel_id=1, source_target_pairs={{0,2},{1,3},{2,0},{3,1},{4,6},{5,7},{6,4},{7,5},{8,10},{9,11},{10,... | collective-permute-start | bytes 147464 | tf_op jit(solution)/shard_map/ppermute | solution.py:137
  1363.6 20.7 %collective-permute-done.139 = f32[3,2,2048]{2,0,1:T(4,128)S(1)} collective-permute-done((f32[3,2,2048]{2,0,1:T(4,128)S(1)}, f32[3,2,2048]{2,0,1:T(4,128)S(1)}, u32[]{:S(2)}, u32[]{:S(2)}) %collective-permute-start.139) | collective-permute-done | bytes 49184 | tf_op jit(solution)/shard_map/ppermute | solution.py:137
  (803 shorter events, 697.7 us)
Async XLA Ops:
  7.2 100.8 %all-gather.8.cloned.1.call-start = ((), (), s32[]{:S(2)}) async-start(), calls=%async_computation.8 | async-start | bytes 7077888 | tf_op jit(solution)/shard_map/all_gather | solution.py:176
  11.6 420.8 %all-gather.14.cloned.1.call-start = ((), (), s32[]{:S(2)}) async-start(), calls=%async_computation.11 | async-start | bytes 2359296 | tf_op jit(solution)/shard_map/all_gather | solution.py:176
  12.4 430.9 %all-gather.12.cloned.1.call-start = ((), (), s32[]{:S(2)}) async-start(), calls=%async_computation.10 | async-start | bytes 5242880 | tf_op jit(solution)/shard_map/all_gather | solution.py:207
  13.2 430.2 %all-gather.10.cloned.1.call-start = ((), (), s32[]{:S(2)}) async-start(), calls=%async_computation.9 | async-start | bytes 9437184 | tf_op jit(solution)/shard_map/all_gather | solution.py:176
  14.6 559.5 %all-gather.18.cloned.1.call-start = ((), (), s32[]{:S(2)}) async-start(), calls=%async_computation.21 | async-start | bytes 5242880 | tf_op jit(solution)/shard_map/all_gather | solution.py:221
  15.1 605.3 %all-gather.16.cloned.1.call-start = ((), (), s32[]{:S(2)}) async-start(), calls=%async_computation.12 | async-start | bytes 9437184 | tf_op jit(solution)/shard_map/all_gather | solution.py:176
  32.2 198.9 %collective-permute-start.25 = (bf16[512,256]{1,0:T(8,128)(2,1)}, bf16[512,256]{1,0:T(8,128)(2,1)}, u32[]{:S(2)}, u32[]{:S(2)}) collective-permute-start(bf16[512,256]{1,0:T(8,128)(2,1)} %get-tuple-element.85), channel_id=1, source_target_pairs={{0,4},{4,8},{8,12},{12,16},{16,20},{20,24},{24,28},{28,0},{1,5},{5... | collective-permute-start | bytes 786440 | tf_op jit(solution)/shard_map/ppermute | solution.py:24
  35.0 1103.7 %reduce-scatter.13.cloned.1.call-start = ((), (), s32[]{:S(2)}) async-start(), calls=%async_computation.15 | async-start | bytes 9437184 | tf_op jit(solution)/shard_map/reduce_scatter | solution.py:184
  136.8 45.2 %collective-permute-start.38 = (bf16[128,2048]{1,0:T(8,128)(2,1)S(1)}, bf16[128,2048]{1,0:T(8,128)(2,1)S(1)}, u32[]{:S(2)}, u32[]{:S(2)}) collective-permute-start(bf16[128,2048]{1,0:T(8,128)(2,1)S(1)} %get-tuple-element.153), channel_id=1, source_target_pairs={{0,1},{4,5},{8,9},{12,13},{16,17},{20,21},{24,25},{28,29}} | collective-permute-start | bytes 1572872 | tf_op jit(solution)/shard_map/ppermute | solution.py:74
  138.1 43.9 %collective-permute-start.41 = (bf16[128,2048]{1,0:T(8,128)(2,1)S(1)}, bf16[128,2048]{1,0:T(8,128)(2,1)S(1)}, u32[]{:S(2)}, u32[]{:S(2)}) collective-permute-start(bf16[128,2048]{1,0:T(8,128)(2,1)S(1)} %get-tuple-element.154), channel_id=1, source_target_pairs={{3,2},{7,6},{11,10},{15,14},{19,18},{23,22},{27,26},{31,30}} | collective-permute-start | bytes 1572872 | tf_op jit(solution)/shard_map/ppermute | solution.py:75
  160.8 43.8 %collective-permute-start.14 = (bf16[128,2048]{1,0:T(8,128)(2,1)}, bf16[128,2048]{1,0:T(8,128)(2,1)}, u32[]{:S(2)}, u32[]{:S(2)}) collective-permute-start(bf16[128,2048]{1,0:T(8,128)(2,1)} %get-tuple-element.145), channel_id=1, source_target_pairs={{0,1},{1,2},{4,5},{5,6},{8,9},{9,10},{12,13},{13,14},{16,17},{17,1... | collective-permute-start | bytes 1572872 | tf_op jit(solution)/shard_map/ppermute | solution.py:74
  166.1 38.4 %collective-permute-start.17 = (bf16[128,2048]{1,0:T(8,128)(2,1)}, bf16[128,2048]{1,0:T(8,128)(2,1)}, u32[]{:S(2)}, u32[]{:S(2)}) collective-permute-start(bf16[128,2048]{1,0:T(8,128)(2,1)} %get-tuple-element.146), channel_id=1, source_target_pairs={{2,1},{3,2},{6,5},{7,6},{10,9},{11,10},{14,13},{15,14},{18,17},{19... | collective-permute-start | bytes 1572872 | tf_op jit(solution)/shard_map/ppermute | solution.py:75
  183.3 39.6 %collective-permute-start.39 = (bf16[128,2048]{1,0:T(8,128)(2,1)}, bf16[128,2048]{1,0:T(8,128)(2,1)}, u32[]{:S(2)}, u32[]{:S(2)}) collective-permute-start(bf16[128,2048]{1,0:T(8,128)(2,1)} %get-tuple-element.151), channel_id=1, source_target_pairs={{0,1},{1,2},{4,5},{5,6},{8,9},{9,10},{12,13},{13,14},{16,17},{17,1... | collective-permute-start | bytes 1572872 | tf_op jit(solution)/shard_map/ppermute | solution.py:74
  239.4 64.8 %collective-permute-start.62 = (bf16[2048,256]{1,0:T(8,128)(2,1)}, bf16[2048,256]{1,0:T(8,128)(2,1)}, u32[]{:S(2)}, u32[]{:S(2)}) collective-permute-start(bf16[2048,256]{1,0:T(8,128)(2,1)} %get-tuple-element.77), channel_id=1, source_target_pairs={{0,4},{4,8},{8,12},{12,16},{16,20},{20,24},{24,28},{28,0},{1,5},{5... | collective-permute-start | bytes 3145736 | tf_op jit(solution)/shard_map/ppermute | solution.py:24
  239.4 70.2 %collective-permute-start.63 = (bf16[2048,256]{1,0:T(8,128)(2,1)}, bf16[2048,256]{1,0:T(8,128)(2,1)}, u32[]{:S(2)}, u32[]{:S(2)}) collective-permute-start(bf16[2048,256]{1,0:T(8,128)(2,1)} %get-tuple-element.77), channel_id=1, source_target_pairs={{0,28},{4,0},{8,4},{12,8},{16,12},{20,16},{24,20},{28,24},{1,29},{... | collective-permute-start | bytes 3145736 | tf_op jit(solution)/shard_map/ppermute | solution.py:29
  242.5 48.1 %collective-permute-start.28 = (bf16[512,256]{1,0:T(8,128)(2,1)S(1)}, bf16[512,256]{1,0:T(8,128)(2,1)S(1)}, u32[]{:S(2)}, u32[]{:S(2)}) collective-permute-start(bf16[512,256]{1,0:T(8,128)(2,1)S(1)} %collective-permute-done.26), channel_id=1, source_target_pairs={{0,28},{4,0},{8,4},{12,8},{16,12},{20,16},{24,20},{28,24},{1,29},{... | collective-permute-start | bytes 786440 | tf_op jit(solution)/shard_map/ppermute | solution.py:29
  244.0 50.9 %collective-permute-start.29 = (bf16[512,256]{1,0:T(8,128)(2,1)S(1)}, bf16[512,256]{1,0:T(8,128)(2,1)S(1)}, u32[]{:S(2)}, u32[]{:S(2)}) collective-permute-start(bf16[512,256]{1,0:T(8,128)(2,1)S(1)} %collective-permute-done.27), channel_id=1, source_target_pairs={{0,4},{4,8},{8,12},{12,16},{16,20},{20,24},{24,28},{28,0},{1,5},{5... | collective-permute-start | bytes 786440 | tf_op jit(solution)/shard_map/ppermute | solution.py:24
  251.1 60.3 %collective-permute-start.20 = (bf16[128,2048]{1,0:T(8,128)(2,1)S(1)}, bf16[128,2048]{1,0:T(8,128)(2,1)S(1)}, u32[]{:S(2)}, u32[]{:S(2)}) collective-permute-start(bf16[128,2048]{1,0:T(8,128)(2,1)S(1)} %get-tuple-element.174), channel_id=1, source_target_pairs={{1,0},{2,1},{3,2},{5,4},{6,5},{7,6},{9,8},{10,9},{11,10},{13,12},{... | collective-permute-start | bytes 1572872 | tf_op jit(solution)/shard_map/ppermute | solution.py:61
  312.7 39.4 %collective-permute-start.23 = (bf16[128,2048]{1,0:T(8,128)(2,1)S(1)}, bf16[128,2048]{1,0:T(8,128)(2,1)S(1)}, u32[]{:S(2)}, u32[]{:S(2)}) collective-permute-start(bf16[128,2048]{1,0:T(8,128)(2,1)S(1)} %collective-permute-done.19), channel_id=1, source_target_pairs={{1,2},{2,3},{5,6},{6,7},{9,10},{10,11},{13,14},{14,15},{17,18},{18... | collective-permute-start | bytes 1572872 | tf_op jit(solution)/shard_map/ppermute | solution.py:60
  318.2 169.7 %collective-permute-start.64 = (bf16[2048,256]{1,0:T(8,128)(2,1)}, bf16[2048,256]{1,0:T(8,128)(2,1)}, u32[]{:S(2)}, u32[]{:S(2)}) collective-permute-start(bf16[2048,256]{1,0:T(8,128)(2,1)} %collective-permute-done.62), channel_id=1, source_target_pairs={{0,4},{4,8},{8,12},{12,16},{16,20},{20,24},{24,28},{28,0},{1,5},{5... | collective-permute-start | bytes 3145736 | tf_op jit(solution)/shard_map/ppermute | solution.py:24
  318.3 59.7 %collective-permute-start.46 = (bf16[128,2048]{1,0:T(8,128)(2,1)S(1)}, bf16[128,2048]{1,0:T(8,128)(2,1)S(1)}, u32[]{:S(2)}, u32[]{:S(2)}) collective-permute-start(bf16[128,2048]{1,0:T(8,128)(2,1)S(1)} %collective-permute-done.45), channel_id=1, source_target_pairs={{1,0},{2,1},{5,4},{6,5},{9,8},{10,9},{13,12},{14,13},{17,16},{18,1... | collective-permute-start | bytes 1572872 | tf_op jit(solution)/shard_map/ppermute | solution.py:61
  323.6 55.1 %collective-permute-start.48 = (bf16[128,2048]{1,0:T(8,128)(2,1)S(1)}, bf16[128,2048]{1,0:T(8,128)(2,1)S(1)}, u32[]{:S(2)}, u32[]{:S(2)}) collective-permute-start(bf16[128,2048]{1,0:T(8,128)(2,1)S(1)} %collective-permute-done.44), channel_id=1, source_target_pairs={{1,2},{2,3},{5,6},{6,7},{9,10},{10,11},{13,14},{14,15},{17,18},{18... | collective-permute-start | bytes 1572872 | tf_op jit(solution)/shard_map/ppermute | solution.py:60
  347.1 167.2 %collective-permute-start.65 = (bf16[2048,256]{1,0:T(8,128)(2,1)}, bf16[2048,256]{1,0:T(8,128)(2,1)}, u32[]{:S(2)}, u32[]{:S(2)}) collective-permute-start(bf16[2048,256]{1,0:T(8,128)(2,1)} %collective-permute-done.63), channel_id=1, source_target_pairs={{0,28},{4,0},{8,4},{12,8},{16,12},{20,16},{24,20},{28,24},{1,29},{... | collective-permute-start | bytes 3145736 | tf_op jit(solution)/shard_map/ppermute | solution.py:29
  352.1 67.0 %collective-permute-start.22 = (bf16[128,2048]{1,0:T(8,128)(2,1)S(1)}, bf16[128,2048]{1,0:T(8,128)(2,1)S(1)}, u32[]{:S(2)}, u32[]{:S(2)}) collective-permute-start(bf16[128,2048]{1,0:T(8,128)(2,1)S(1)} %collective-permute-done.21), channel_id=1, source_target_pairs={{1,0},{5,4},{9,8},{13,12},{17,16},{21,20},{25,24},{29,28}} | collective-permute-start | bytes 1572872 | tf_op jit(solution)/shard_map/ppermute | solution.py:61
  378.1 42.5 %collective-permute-start.24 = (bf16[128,2048]{1,0:T(8,128)(2,1)S(1)}, bf16[128,2048]{1,0:T(8,128)(2,1)S(1)}, u32[]{:S(2)}, u32[]{:S(2)}) collective-permute-start(bf16[128,2048]{1,0:T(8,128)(2,1)S(1)} %collective-permute-done.23), channel_id=1, source_target_pairs={{2,3},{6,7},{10,11},{14,15},{18,19},{22,23},{26,27},{30,31}} | collective-permute-start | bytes 1572872 | tf_op jit(solution)/shard_map/ppermute | solution.py:60
  378.8 51.9 %collective-permute-start.47 = (bf16[128,2048]{1,0:T(8,128)(2,1)S(1)}, bf16[128,2048]{1,0:T(8,128)(2,1)S(1)}, u32[]{:S(2)}, u32[]{:S(2)}) collective-permute-start(bf16[128,2048]{1,0:T(8,128)(2,1)S(1)} %collective-permute-done.46), channel_id=1, source_target_pairs={{1,0},{5,4},{9,8},{13,12},{17,16},{21,20},{25,24},{29,28}} | collective-permute-start | bytes 1572872 | tf_op jit(solution)/shard_map/ppermute | solution.py:61
  517.9 44.4 %collective-permute-start.68 = (bf16[2048,256]{1,0:T(8,128)(2,1)S(1)}, bf16[2048,256]{1,0:T(8,128)(2,1)S(1)}, u32[]{:S(2)}, u32[]{:S(2)}) collective-permute-start(bf16[2048,256]{1,0:T(8,128)(2,1)S(1)} %collective-permute-done.66), channel_id=1, source_target_pairs={{0,4},{4,8},{8,12},{12,16},{16,20},{20,24},{24,28},{28,0},{1,5},{5... | collective-permute-start | bytes 3145736 | tf_op jit(solution)/shard_map/ppermute | solution.py:24
  583.9 62.6 %collective-permute-start.72 = (bf16[128,2048]{1,0:T(8,128)(2,1)}, bf16[128,2048]{1,0:T(8,128)(2,1)}, u32[]{:S(2)}, u32[]{:S(2)}) collective-permute-start(bf16[128,2048]{1,0:T(8,128)(2,1)} %collective-permute-done.71), channel_id=1, source_target_pairs={{1,0},{5,4},{9,8},{13,12},{17,16},{21,20},{25,24},{29,28}} | collective-permute-start | bytes 1572872 | tf_op jit(solution)/shard_map/ppermute | solution.py:61
  598.4 49.3 %collective-permute-start.74 = (bf16[128,2048]{1,0:T(8,128)(2,1)}, bf16[128,2048]{1,0:T(8,128)(2,1)}, u32[]{:S(2)}, u32[]{:S(2)}) collective-permute-start(bf16[128,2048]{1,0:T(8,128)(2,1)} %collective-permute-done.73), channel_id=1, source_target_pairs={{2,3},{6,7},{10,11},{14,15},{18,19},{22,23},{26,27},{30,31}} | collective-permute-start | bytes 1572872 | tf_op jit(solution)/shard_map/ppermute | solution.py:60
  679.0 462.5 %reduce-scatter.11.cloned.1.call-start = ((), (), s32[]{:S(2)}) async-start(), calls=%async_computation.14 | async-start | bytes 9437184 | tf_op jit(solution)/shard_map/reduce_scatter | solution.py:187
  693.5 542.0 %reduce-scatter.15.cloned.1.call-start = ((), (), s32[]{:S(2)}) async-start(), calls=%async_computation.16 | async-start | bytes 2359296 | tf_op jit(solution)/shard_map/reduce_scatter | solution.py:187
  849.0 388.2 %reduce-scatter.17.cloned.1.call-start = ((), (), s32[]{:S(2)}) async-start(), calls=%async_computation.17 | async-start | bytes 2359296 | tf_op jit(solution)/shard_map/reduce_scatter | solution.py:184
  889.7 392.2 %reduce-scatter.9.cloned.1.call-start = ((), (), s32[]{:S(2)}) async-start(), calls=%async_computation.13 | async-start | bytes 5242880 | tf_op jit(solution)/shard_map/reduce_scatter | solution.py:255
  909.8 374.7 %reduce-scatter.23.cloned.1.call-start = ((), (), s32[]{:S(2)}) async-start(), calls=%async_computation.20 | async-start | bytes 2359296 | tf_op jit(solution)/shard_map/reduce_scatter | solution.py:187
  949.2 42.3 %collective-permute-start.106 = (bf16[128,2048]{1,0:T(8,128)(2,1)}, bf16[128,2048]{1,0:T(8,128)(2,1)}, u32[]{:S(2)}, u32[]{:S(2)}) collective-permute-start(bf16[128,2048]{1,0:T(8,128)(2,1)} %get-tuple-element.119), channel_id=1, source_target_pairs={{0,1},{1,2},{4,5},{5,6},{8,9},{9,10},{12,13},{13,14},{16,17},{17,1... | collective-permute-start | bytes 1572872 | tf_op jit(solution)/shard_map/ppermute | solution.py:74
  966.3 43.5 %collective-permute-start.89 = (bf16[128,2048]{1,0:T(8,128)(2,1)}, bf16[128,2048]{1,0:T(8,128)(2,1)}, u32[]{:S(2)}, u32[]{:S(2)}) collective-permute-start(bf16[128,2048]{1,0:T(8,128)(2,1)} %get-tuple-element.105), channel_id=1, source_target_pairs={{0,1},{1,2},{2,3},{4,5},{5,6},{6,7},{8,9},{9,10},{10,11},{12,13},{... | collective-permute-start | bytes 1572872 | tf_op jit(solution)/shard_map/ppermute | solution.py:74
  1033.4 44.0 %collective-permute-start.118 = (bf16[128,2048]{1,0:T(8,128)(2,1)S(1)}, bf16[128,2048]{1,0:T(8,128)(2,1)S(1)}, u32[]{:S(2)}, u32[]{:S(2)}) collective-permute-start(bf16[128,2048]{1,0:T(8,128)(2,1)S(1)} %get-tuple-element.68), channel_id=1, source_target_pairs={{1,0},{2,1},{3,2},{5,4},{6,5},{7,6},{9,8},{10,9},{11,10},{13,12},{... | collective-permute-start | bytes 1572872 | tf_op jit(solution)/shard_map/ppermute | solution.py:61
  1034.8 43.9 %collective-permute-start.117 = (bf16[128,2048]{1,0:T(8,128)(2,1)S(1)}, bf16[128,2048]{1,0:T(8,128)(2,1)S(1)}, u32[]{:S(2)}, u32[]{:S(2)}) collective-permute-start(bf16[128,2048]{1,0:T(8,128)(2,1)S(1)} %get-tuple-element.68), channel_id=1, source_target_pairs={{0,1},{1,2},{2,3},{4,5},{5,6},{6,7},{8,9},{9,10},{10,11},{12,13},{... | collective-permute-start | bytes 1572872 | tf_op jit(solution)/shard_map/ppermute | solution.py:60
  1131.2 188.9 %reduce-scatter.19.cloned.1.call-start = ((), (), s32[]{:S(2)}) async-start(), calls=%async_computation.18 | async-start | bytes 9437184 | tf_op jit(solution)/shard_map/reduce_scatter | solution.py:184
  1131.9 256.4 %reduce-scatter.21.cloned.1.call-start = ((), (), s32[]{:S(2)}) async-start(), calls=%async_computation.19 | async-start | bytes 7077888 | tf_op jit(solution)/shard_map/reduce_scatter | solution.py:184
  1206.2 43.0 %collective-permute-start.129 = (bf16[128,4096]{1,0:T(8,128)(2,1)}, bf16[128,4096]{1,0:T(8,128)(2,1)}, u32[]{:S(2)}, u32[]{:S(2)}) collective-permute-start(bf16[128,4096]{1,0:T(8,128)(2,1)} %dynamic-slice_bitcast_fusion.1), channel_id=1, source_target_pairs={{0,1},{4,5},{8,9},{12,13},{16,17},{20,21},{24,25},{28,29}} | collective-permute-start | bytes 3145736 | tf_op jit(solution)/shard_map/ppermute | solution.py:74
  1228.3 43.4 %collective-permute-start.124 = (bf16[256,2048]{1,0:T(8,128)(2,1)}, bf16[256,2048]{1,0:T(8,128)(2,1)}, u32[]{:S(2)}, u32[]{:S(2)}) collective-permute-start(bf16[256,2048]{1,0:T(8,128)(2,1)} %get-tuple-element.90), channel_id=1, source_target_pairs={{0,1},{1,2},{4,5},{5,6},{8,9},{9,10},{12,13},{13,14},{16,17},{17,1... | collective-permute-start | bytes 3145736 | tf_op jit(solution)/shard_map/ppermute | solution.py:74
  1233.7 38.0 %collective-permute-start.127 = (bf16[256,2048]{1,0:T(8,128)(2,1)S(1)}, bf16[256,2048]{1,0:T(8,128)(2,1)}, u32[]{:S(2)}, u32[]{:S(2)}) collective-permute-start(bf16[256,2048]{1,0:T(8,128)(2,1)S(1)} %get-tuple-element.91), channel_id=1, source_target_pairs={{2,1},{3,2},{6,5},{7,6},{10,9},{11,10},{14,13},{15,14},{18,17},{19... | collective-permute-start | bytes 3145736 | tf_op jit(solution)/shard_map/ppermute | solution.py:75
  1252.0 42.2 %collective-permute-start.130 = (bf16[128,4096]{1,0:T(8,128)(2,1)}, bf16[128,4096]{1,0:T(8,128)(2,1)}, u32[]{:S(2)}, u32[]{:S(2)}) collective-permute-start(bf16[128,4096]{1,0:T(8,128)(2,1)} %fusion.150), channel_id=1, source_target_pairs={{0,1},{1,2},{4,5},{5,6},{8,9},{9,10},{12,13},{13,14},{16,17},{17,1... | collective-permute-start | bytes 3145736 | tf_op jit(solution)/shard_map/ppermute | solution.py:74
  1276.1 40.5 %collective-permute-start.125 = (bf16[256,2048]{1,0:T(8,128)(2,1)}, bf16[256,2048]{1,0:T(8,128)(2,1)S(1)}, u32[]{:S(2)}, u32[]{:S(2)}) collective-permute-start(bf16[256,2048]{1,0:T(8,128)(2,1)} %get-tuple-element.88), channel_id=1, source_target_pairs={{0,1},{1,2},{2,3},{4,5},{5,6},{6,7},{8,9},{9,10},{10,11},{12,13},{... | collective-permute-start | bytes 3145736 | tf_op jit(solution)/shard_map/ppermute | solution.py:74
  1297.3 87.7 %collective-permute-start.131 = (bf16[128,4096]{1,0:T(8,128)(2,1)}, bf16[128,4096]{1,0:T(8,128)(2,1)}, u32[]{:S(2)}, u32[]{:S(2)}) collective-permute-start(bf16[128,4096]{1,0:T(8,128)(2,1)} %get-tuple-element.64), channel_id=1, source_target_pairs={{0,1},{1,2},{2,3},{4,5},{5,6},{6,7},{8,9},{9,10},{10,11},{12,13},{... | collective-permute-start | bytes 3145736 | tf_op jit(solution)/shard_map/ppermute | solution.py:74
  1338.4 46.6 %collective-permute-start.134 = (bf16[128,4096]{1,0:T(8,128)(2,1)}, bf16[128,4096]{1,0:T(8,128)(2,1)}, u32[]{:S(2)}, u32[]{:S(2)}) collective-permute-start(bf16[128,4096]{1,0:T(8,128)(2,1)} %add_convert_fusion), channel_id=1, source_target_pairs={{1,0},{2,1},{3,2},{5,4},{6,5},{7,6},{9,8},{10,9},{11,10},{13,12},{... | collective-permute-start | bytes 3145736 | tf_op jit(solution)/shard_map/ppermute | solution.py:75
  1341.6 42.8 %collective-permute-start.139 = (f32[3,2,2048]{2,0,1:T(4,128)S(1)}, f32[3,2,2048]{2,0,1:T(4,128)S(1)}, u32[]{:S(2)}, u32[]{:S(2)}) collective-permute-start(f32[3,2,2048]{2,0,1:T(4,128)S(1)} %add.682), channel_id=1, source_target_pairs={{0,2},{1,3},{2,0},{3,1},{4,6},{5,7},{6,4},{7,5},{8,10},{9,11},{10,... | collective-permute-start | bytes 147464 | tf_op jit(solution)/shard_map/ppermute | solution.py:137
  (240 other events, 6053.5 us)
Sparse Core Ops, SparseCore 0:
  11.7 55.6 all-gather.7
  69.4 29.1 all-gather.13
  100.2 118.6 all-gather.11
  220.6 84.7 all-gather.9
  306.8 113.3 all-gather.17
  421.9 52.3 all-gather.15
  679.2 76.1 reduce-scatter.12
  758.9 71.2 reduce-scatter.10
  849.2 47.8 reduce-scatter.14
  900.2 41.0 reduce-scatter.16
  943.6 116.5 reduce-scatter.8
  1131.3 42.5 reduce-scatter.22
  1177.3 71.3 reduce-scatter.18
  1252.0 61.7 reduce-scatter.20
